TPU v7x, 32 devices: a whole 2x2x4 slice. The times are simulated.
32 devices in a mesh: member: 2 (over y), gy: 4 (over z), gx: 2 (over x), lev: 2 (over core).
Axes of the slice: x: 2, y: 2, z: 4, core: 2. Of those that a mesh axis runs over, the one named last changes fastest.
Arguments:
- level_field: bfloat16 [32, 1536, 1536], P(('member', 'lev'), 'gy', 'gx'), parts along dimension 0, may hold values from -6 to 6
Outputs:
- spectra: float32 [1536, 32, 1536], P(('gy', 'gx'), ('member', 'lev')), parts along dimension 1
- spectra_zone: float32 [1536, 32, 11], P(('gy', 'gx'), ('member', 'lev')), parts along dimension 1
There are 2 independent parts, one for each index of `member`. A program takes and returns all parts, laid end to end along the dimension named above; each array names one. Nothing has to cross between parts.
All inputs are finite; a program needn't handle non-finite values.
Results may differ from a plain program's by a relative error of at most 0.0042.
Values may be sent and summed in bfloat16 or wider, within the bound.
A program may use at most 128 MiB of HBM per device.

v0:
```python
import math
import jax
import jax.numpy as jnp
from jax import lax
from jax.sharding import PartitionSpec as P

NX = 1536
NY = 1536
EXT_ZONE = 11
WAVES = 768


def blend_zone(second_last, last_value, first_value, second_value, zone_count):
    steps = (jnp.arange(zone_count, dtype=jnp.int32) + 1).astype(jnp.float32) / (zone_count + 1.0)
    weight_a = 2.0 * steps**3 - 3.0 * steps**2 + 1.0
    weight_b = steps**3 - 2.0 * steps**2 + steps
    weight_c = -2.0 * steps**3 + 3.0 * steps**2
    weight_d = steps**3 - steps**2
    tangent_scale = zone_count + 1.0
    slope_start = tangent_scale * (last_value - second_last)
    slope_end = tangent_scale * (second_value - first_value)
    return (
        last_value[..., None] * weight_a
        + slope_start[..., None] * weight_b
        + first_value[..., None] * weight_c
        + slope_end[..., None] * weight_d
    )


def make_table(wave_count, length):
    coeff = jnp.arange(2 * wave_count, dtype=jnp.int32)[:, None]
    column = jnp.arange(length, dtype=jnp.int32)[None, :]
    is_cosine = coeff < wave_count
    number = jnp.where(is_cosine, coeff, coeff - wave_count + 1)
    phase = (number * column % length).astype(jnp.float32) * (2.0 * math.pi / length)
    values = jnp.where(is_cosine, jnp.cos(phase), -jnp.sin(phase)) / math.sqrt(length)
    return values.astype(jnp.bfloat16)


def shards(level_field):
    wave_table = make_table(WAVES, NX + EXT_ZONE)
    core_table = wave_table[:, :NX]
    zone_table = wave_table[:, NX:]
    core_rows = lax.all_to_all(level_field, "gx", split_axis=1, concat_axis=2, tiled=True)
    widened = core_rows.astype(jnp.float32)
    zone_cols = blend_zone(
        widened[..., NX - 2], widened[..., NX - 1], widened[..., 0], widened[..., 1], EXT_ZONE
    ).astype(jnp.bfloat16)
    dims = (((1,), (2,)), ((), ()))
    total = lax.dot_general(core_table, core_rows, dims, preferred_element_type=jnp.float32)
    partial_spec = total + lax.dot_general(
        zone_table, zone_cols, dims, preferred_element_type=jnp.float32
    )
    moved = lax.all_to_all(partial_spec, ("gy", "gx"), split_axis=0, concat_axis=2, tiled=True)
    spectra_zone = blend_zone(
        moved[..., NY - 2], moved[..., NY - 1], moved[..., 0], moved[..., 1], EXT_ZONE
    )
    return (moved, spectra_zone)


def solution(mesh):
    return jax.shard_map(
        shards,
        mesh=mesh,
        in_specs=(P(("member", "lev"), "gy", "gx"),),
        out_specs=(
            P(("gy", "gx"), ("member", "lev"), None),
            P(("gy", "gx"), ("member", "lev"), None),
        ),
        check_vma=False,
    )
```

profile of v0, /device:TPU:0, one launch (start us, length us, event | category | flops | bytes accessed | tf_op | source)
XLA Modules:
  0.0 426.6 jit_solution(1554581682853218261)
XLA Ops:
  0.6 7.1 %copy.14 = bf16[8,384,768]{2,0,1:T(8,128)(2,1)} copy(bf16[8,384,768]{2,1,0:T(8,128)(2,1)} %param.1) | data formatting | bytes 9437184 | tf_op args[0]
  7.8 6.0 %all-to-all-start = ((bf16[8,384,768]{2,0,1:T(8,128)(2,1)}), bf16[8,384,768]{2,0,1:T(8,128)(2,1)}, u32[]{:S(2)}, u32[]{:S(2)}) async-start(bf16[8,384,768]{2,0,1:T(8,128)(2,1)} %copy.14), calls=%async_computation | async-start | bytes 9437184 | tf_op jit(solution)/shard_map/all_to_all | solution.py:44
  13.8 46.7 %multiply_convert_fusion = bf16[1536,1547]{1,0:T(8,128)(2,1)} fusion(s32[1536]{0:T(1024)S(1)} %add_select_fusion.1, pred[1536]{0:T(1024)(128)(4,1)S(1)} %iota_compare_fusion), kind=kLoop, calls=%fused_computation.3 | loop fusion | flops 30890496 | bytes 4760064 | tf_op jit(solution)/shard_map/convert_element_type | solution.py:37
  60.5 7.7 %all-to-all-done = bf16[8,384,768]{2,0,1:T(8,128)(2,1)} async-done(((bf16[8,384,768]{2,0,1:T(8,128)(2,1)}), bf16[8,384,768]{2,0,1:T(8,128)(2,1)}, u32[]{:S(2)}, u32[]{:S(2)}) %all-to-all-start) | async-done | bytes 4718624 | tf_op jit(solution)/shard_map/all_to_all | solution.py:44
  68.2 9.4 %copy.23 = bf16[8,2,192,768]{3,1,2,0:T(2,128)(2,1)} copy(bf16[8,2,192,768]{3,0,2,1:T(8,128)(2,1)} %bitcast.1) | data formatting | bytes 9437184 | tf_op jit(solution)/shard_map/all_to_all | solution.py:44
  77.6 0.0 slice-start.2
  77.6 11.3 %all_to_all.29 = bf16[8,192,1536]{2,1,0:T(8,128)(2,1)} reshape(bf16[8,192,2,768]{3,2,1,0:T(2,128)(2,1)} %bitcast.28) | data formatting | bytes 9437184 | tf_op jit(solution)/shard_map/all_to_all | solution.py:44
  88.9 0.0 slice-start.3
  88.9 3.8 convert_element_type.49
  92.7 0.0 slice-start
  92.7 1.8 slice_reduce_fusion.1
  94.5 0.0 slice-done.2
  94.5 0.0 slice-done.3
  94.6 0.0 slice-start.1
  94.6 1.5 fusion.9
  96.1 0.0 slice-done
  96.1 0.0 slice-done.1
  96.1 10.6 %convolution_add_fusion = f32[1536,8,192]{0,2,1:T(8,128)} fusion(f32[1536,8,192]{0,2,1:T(8,128)S(1)} %fusion.9, bf16[8,192,1536]{2,1,0:T(8,128)(2,1)S(1)} %bitcast.27, bf16[1536,1547]{1,0:T(8,128)(2,1)S(1)} %bitcast.30), kind=kOutput, calls=%fused_computation.8 | convolution fusion | flops 7250116608 | bytes 28311552 | tf_op jit(solution)/shard_map/dot_general | solution.py:50
  106.7 12.8 %copy.17 = f32[1536,8,192]{2,1,0:T(8,128)} copy(f32[1536,8,192]{0,2,1:T(8,128)} %convolution_add_fusion) | data formatting | bytes 18874368 | tf_op jit(solution)/shard_map/add | solution.py:51
  119.5 279.9 %all_to_all.36 = f32[1536,8,192]{2,1,0:T(8,128)} all-to-all(f32[1536,8,192]{2,1,0:T(8,128)} %copy.17), channel_id=1, replica_groups=mesh['member'=2,'gy'=4,'gx'=2,'lev'=2] {'gy','gx'}, dimensions={0} | all-to-all | bytes 18874368 | tf_op jit(solution)/shard_map/all_to_all | solution.py:54
  399.4 13.8 %copy.18 = f32[8,192,8,192]{1,2,3,0:T(8,128)} copy(f32[8,192,8,192]{3,2,1,0:T(8,128)} %bitcast.25) | data formatting | bytes 18874368 | tf_op jit(solution)/shard_map/all_to_all | solution.py:54
  413.2 0.8 slice_bitcast_fusion.5
  414.0 11.9 %copy.19 = f32[192,8,1536]{2,1,0:T(8,128)} copy(f32[192,8,1536]{0,1,2:T(8,128)} %bitcast.24) | data formatting | bytes 18874368
  425.9 0.8 multiply_add_fusion
  (6 shorter events, 0.0 us)
Async XLA Ops:
  7.8 60.5 %all-to-all-start = ((bf16[8,384,768]{2,0,1:T(8,128)(2,1)}), bf16[8,384,768]{2,0,1:T(8,128)(2,1)}, u32[]{:S(2)}, u32[]{:S(2)}) async-start(bf16[8,384,768]{2,0,1:T(8,128)(2,1)} %copy.14), calls=%async_computation | async-start | bytes 9437184 | tf_op jit(solution)/shard_map/all_to_all | solution.py:44
  77.6 16.9 %slice-start.2 = ((s8[5111808]{0:T(1024)(128)(4,1)}), s8[917504]{0:T(1024)(128)(4,1)S(1)}, s32[]{:S(2)}) async-start(s8[5111808]{0:T(1024)(128)(4,1)} %bitcast.29), calls=%async_computation.4 | async-start | bytes 1835008
  88.9 5.6 %slice-start.3 = ((s8[5111808]{0:T(1024)(128)(4,1)}), s8[4194304]{0:T(1024)(128)(4,1)S(1)}, s32[]{:S(2)}) async-start(s8[5111808]{0:T(1024)(128)(4,1)} %bitcast.29), calls=%async_computation.5 | async-start | bytes 8388608
  92.7 3.4 slice-start
  94.6 1.5 slice-start.1
where the time goes:
time: 428 us; the launch traced here: 427 us
  blocking collectives  280 us (65%)
  local copies, waits for them, and re-layouts  66.3 us (15%)
  other arithmetic  53.8 us (13%)
  matrix products  12.1 us (3%)
  waiting for transfers between devices  7.74 us (2%)
  starting transfers between devices  5.95 us (1%)
    all_to_all x1, blocking collectives, shards(): lax.all_to_all(partial_spec, ('gy', 'gx'), split_axis=0, concat_axis=2, t...  280 us
    convert_element_type x1, other arithmetic, make_table(): return values.astype(jnp.bfloat16)  46.7 us
    all_to_all x2, local copies, waits for them, and re-layouts, shards(): lax.all_to_all(level_field, 'gx', split_axis=1, concat_axis=2, tiled=True)  20.7 us
    unnamed x10, local copies, waits for them, and re-layouts  19 us
    all_to_all x1, local copies, waits for them, and re-layouts, shards(): lax.all_to_all(partial_spec, ('gy', 'gx'), split_axis=0, concat_axis=2, t...  13.8 us
    add x1, local copies, waits for them, and re-layouts, shards(): total + lax.dot_general(zone_table, zone_cols, dims, preferred_element_ty...  12.8 us
    dot_general x1, matrix products, shards(): lax.dot_general(core_table, core_rows, dims, preferred_element_type=jnp.f...  10.6 us
  transfers between devices with their start and end apart: 1, of which 1 were waited for; matrix products, arithmetic and copies ran while one was open for 11% of the time, Pallas kernels for 0%

commit v1 on v0

--- a/solution.py
+++ b/solution.py
@@ -41,7 +41,10 @@
     wave_table = make_table(WAVES, NX + EXT_ZONE)
     core_table = wave_table[:, :NX]
     zone_table = wave_table[:, NX:]
-    core_rows = lax.all_to_all(level_field, "gx", split_axis=1, concat_axis=2, tiled=True)
+    core_rows = jnp.concatenate(
+        lax.all_to_all(jnp.stack(jnp.split(level_field, lax.axis_size("gx"), axis=1)), "gx", 0, 0),
+        axis=2,
+    )
     widened = core_rows.astype(jnp.float32)
     zone_cols = blend_zone(
         widened[..., NX - 2], widened[..., NX - 1], widened[..., 0], widened[..., 1], EXT_ZONE

time: 428 us -> 405 us (0.946)
  local copies, waits for them, and re-layouts: 66.3 us -> 44 us
    all_to_all x2 -> x0, local copies, waits for them, and re-layouts: 20.7 us -> none  [shards(): lax.all_to_all(level_field, 'gx', split_axis=1, concat_axis=2, tiled=True)]
    unnamed x10 -> x5, local copies, waits for them, and re-layouts: 19 us -> 11.9 us
  transfers between devices with their start and end apart: 1 -> 1, of which waited for: 1 -> 1; matrix products, arithmetic and copies ran while one was open for 11% -> 12% of each run, Pallas kernels for 0% -> 0%
where the time goes in v1:
time: 405 us; the launch traced here: 404 us
  blocking collectives  280 us (69%)
  other arithmetic  53.9 us (13%)
  local copies, waits for them, and re-layouts  44 us (11%)
  matrix products  11.9 us (3%)
  waiting for transfers between devices  7.72 us (2%)
  starting transfers between devices  5.77 us (1%)
    all_to_all x1, blocking collectives, shards(): lax.all_to_all(partial_spec, ('gy', 'gx'), split_axis=0, concat_axis=2, t...  280 us
    convert_element_type x1, other arithmetic, make_table(): return values.astype(jnp.bfloat16)  46.7 us
    all_to_all x1, local copies, waits for them, and re-layouts, shards(): lax.all_to_all(partial_spec, ('gy', 'gx'), split_axis=0, concat_axis=2, t...  13.8 us
    add x1, local copies, waits for them, and re-layouts, shards(): total + lax.dot_general(zone_table, zone_cols, dims, preferred_element_ty...  12.8 us
    unnamed x5, local copies, waits for them, and re-layouts  11.9 us
    dot_general x1, matrix products, shards(): lax.dot_general(core_table, core_rows, dims, preferred_element_type=jnp.f...  10.4 us
  transfers between devices with their start and end apart: 1, of which 1 were waited for; matrix products, arithmetic and copies ran while one was open for 12% of the time, Pallas kernels for 0%

profile of v1, /device:TPU:0, one launch (start us, length us, event | category | flops | bytes accessed | tf_op | source)
XLA Modules:
  0.0 404.0 jit_solution(9415132332485628620)
XLA Ops:
  0.6 2.8 slice_bitcast_fusion.3
  3.4 2.6 pad_maximum_fusion
  6.0 5.8 %all-to-all-start = ((bf16[2,8,192,768]{3,2,1,0:T(8,128)(2,1)}), bf16[2,8,192,768]{3,2,1,0:T(8,128)(2,1)}, u32[]{:S(2)}, u32[]{:S(2)}) async-start(bf16[2,8,192,768]{3,2,1,0:T(8,128)(2,1)} %pad_maximum_fusion), calls=%async_computation | async-start | bytes 9437184 | tf_op jit(solution)/shard_map/all_to_all | solution.py:45
  11.8 46.7 %multiply_convert_fusion = bf16[1536,1547]{1,0:T(8,128)(2,1)} fusion(s32[1536]{0:T(1024)S(1)} %add_select_fusion.1, pred[1536]{0:T(1024)(128)(4,1)S(1)} %iota_compare_fusion), kind=kLoop, calls=%fused_computation.3 | loop fusion | flops 30890496 | bytes 4760064 | tf_op jit(solution)/shard_map/convert_element_type | solution.py:37
  58.5 7.7 %all-to-all-done = bf16[2,8,192,768]{3,2,1,0:T(8,128)(2,1)} async-done(((bf16[2,8,192,768]{3,2,1,0:T(8,128)(2,1)}), bf16[2,8,192,768]{3,2,1,0:T(8,128)(2,1)}, u32[]{:S(2)}, u32[]{:S(2)}) %all-to-all-start) | async-done | bytes 4718624 | tf_op jit(solution)/shard_map/all_to_all | solution.py:45
  66.3 2.7 copy.21
  69.0 0.0 slice-start
  69.0 0.0 slice-start.1
  69.0 1.3 convert_element_type.49
  70.3 1.8 slice_reduce_fusion.1
  72.1 0.0 slice-done
  72.2 0.0 slice-done.1
  72.2 1.5 fusion.9
  73.7 10.4 %convolution_add_fusion = f32[1536,8,192]{0,2,1:T(8,128)} fusion(f32[1536,8,192]{0,2,1:T(8,128)S(1)} %fusion.9, bf16[8,192,1536]{2,1,0:T(8,128)(2,1)S(1)} %bitcast.30, bf16[1536,1547]{1,0:T(8,128)(2,1)S(1)} %bitcast.32), kind=kOutput, calls=%fused_computation.8 | convolution fusion | flops 7250116608 | bytes 28311552 | tf_op jit(solution)/shard_map/dot_general | solution.py:53
  84.1 12.8 %copy.16 = f32[1536,8,192]{2,1,0:T(8,128)} copy(f32[1536,8,192]{0,2,1:T(8,128)} %convolution_add_fusion) | data formatting | bytes 18874368 | tf_op jit(solution)/shard_map/add | solution.py:54
  96.8 280.0 %all_to_all.23 = f32[1536,8,192]{2,1,0:T(8,128)} all-to-all(f32[1536,8,192]{2,1,0:T(8,128)} %copy.16), channel_id=1, replica_groups=mesh['member'=2,'gy'=4,'gx'=2,'lev'=2] {'gy','gx'}, dimensions={0} | all-to-all | bytes 18874368 | tf_op jit(solution)/shard_map/all_to_all | solution.py:57
  376.8 13.8 %copy.17 = f32[8,192,8,192]{1,2,3,0:T(8,128)} copy(f32[8,192,8,192]{3,2,1,0:T(8,128)} %bitcast.28) | data formatting | bytes 18874368 | tf_op jit(solution)/shard_map/all_to_all | solution.py:57
  390.6 0.8 slice_bitcast_fusion.7
  391.4 11.9 %copy.18 = f32[192,8,1536]{2,1,0:T(8,128)} copy(f32[192,8,1536]{0,1,2:T(8,128)} %bitcast.27) | data formatting | bytes 18874368
  403.2 0.8 multiply_add_fusion
  (5 shorter events, 0.0 us)
Async XLA Ops:
  6.0 60.3 %all-to-all-start = ((bf16[2,8,192,768]{3,2,1,0:T(8,128)(2,1)}), bf16[2,8,192,768]{3,2,1,0:T(8,128)(2,1)}, u32[]{:S(2)}, u32[]{:S(2)}) async-start(bf16[2,8,192,768]{3,2,1,0:T(8,128)(2,1)} %pad_maximum_fusion), calls=%async_computation | async-start | bytes 9437184 | tf_op jit(solution)/shard_map/all_to_all | solution.py:45
  69.0 3.1 slice-start
  69.0 3.1 slice-start.1
